TPU v7x, 256 devices: a 4x2x16 block of a 4x16x16 slice. The times are simulated.
256 devices in a mesh: groups: 2 (over y), section: 4 (over x), axial: 32 (over z, core).
Axes of the slice: x: 4, y: 2, z: 16, core: 2. Of those that a mesh axis runs over, the one named last changes fastest.
The devices are a block of a 4x16x16 slice.
Arguments:
- pair_in: bfloat16 [8, 256, 256, 128], P('groups', 'axial'), parts along dimension 0, may hold values from -6 to 6
- crop_mask: int32 [8, 256], P('groups'), parts along dimension 0, may hold values 0 or 1
- proj_weights: bfloat16 [4, 5, 128, 128], P('section'), may hold values from -0.5 to 0.5
- out_weights: bfloat16 [4, 128, 128], P('section'), may hold values from -0.5 to 0.5
- up_weights: bfloat16 [4, 128, 512], P('section'), may hold values from -0.5 to 0.5
- down_weights: bfloat16 [4, 512, 128], P('section'), may hold values from -0.25 to 0.25
- norm_gains: bfloat16 [4, 3, 128], P('section'), may hold values from 0.099609375 to 1.8984375
Outputs:
- pair_out: bfloat16 [8, 256, 256, 128], P(('groups', 'section'), 'axial'), parts along dimension 0
There are 2 independent parts, one for each index of `groups`. A program takes and returns all parts, laid end to end along the dimension named above; an argument that names none is the same for every part. Nothing has to cross between parts.
Inputs may be any that keep to these rules, and one draw needn't show every extreme that they name: `crop_mask`: 1 marks a residue inside the crop, 0 a padded one.
All inputs are finite; a program needn't handle non-finite values.
Results may differ from a plain program's by a relative error of at most 0.013.
Values may be sent and summed in bfloat16 or wider, within the bound.
A program may use at most 64 MiB of HBM per device.

v0:
```python
import jax
import jax.numpy as jnp
from jax import lax
from jax.sharding import PartitionSpec as P

epsilon = 1e-05


def sent_together(arrays, axis, dim, along):
    columns = [a.reshape(*a.shape[:along], -1) for a in arrays]
    both = jnp.concatenate(columns, axis=along)
    result, at, outs = (lax.all_gather(both, axis, axis=dim, tiled=True), 0, [])
    for a, column in zip(arrays, columns):
        section = result[..., at : at + column.shape[along]]
        outs.append(section.reshape(*section.shape[:along], *a.shape[along:]))
        at += column.shape[along]
    return tuple(outs)


def normalize(values, axis_dim):
    center = values - jnp.mean(values, axis=axis_dim, keepdims=True)
    spread = jnp.mean(center * center, axis=axis_dim, keepdims=True)
    return center * lax.rsqrt(spread + epsilon)


def triangle(pieces):
    return jnp.einsum(
        "gcik,gcjk->gcij", pieces[0], pieces[1], preferred_element_type=jnp.float32
    ).astype(jnp.bfloat16)


def evo_block(current, mask_all, proj_mats, out_mat, up_mat, down_mat, gain_rows):
    row_count = current.shape[0]
    width = current.shape[1]
    channels = current.shape[2]
    group_count = lax.axis_size("axial")
    per_group = channels // group_count
    row_start = lax.axis_index("axial") * row_count
    mask_rows = lax.dynamic_slice_in_dim(mask_all, row_start, row_count)
    gain_vals = gain_rows.astype(jnp.float32)
    pair_f = current.astype(jnp.float32)
    normed = (normalize(pair_f, 2) * gain_vals[0]).astype(jnp.bfloat16)
    linear = jnp.einsum("rnd,edc->ecrn", normed, proj_mats[:4], preferred_element_type=jnp.float32)
    pair_mask = mask_rows[:, None] * mask_all[None, :]
    left_edge = (jax.nn.sigmoid(linear[1]) * linear[0] * pair_mask).astype(jnp.bfloat16)
    right_edge = (jax.nn.sigmoid(linear[3]) * linear[2] * pair_mask).astype(jnp.bfloat16)
    left_groups = left_edge.reshape(group_count, per_group, row_count, width)
    right_groups = right_edge.reshape(group_count, per_group, row_count, width)
    product = triangle(
        (
            lax.all_to_all(left_groups, "axial", split_axis=0, concat_axis=2, tiled=True),
            lax.all_to_all(right_groups, "axial", split_axis=0, concat_axis=2, tiled=True),
        )
    )
    restored = lax.all_to_all(product, "axial", split_axis=2, concat_axis=0, tiled=True).reshape(
        channels, row_count, width
    )
    tri_norm = (normalize(restored.astype(jnp.float32), 0) * gain_vals[1][:, None, None]).astype(
        jnp.bfloat16
    )
    update = jnp.einsum("crn,cd->rnd", tri_norm, out_mat, preferred_element_type=jnp.float32)
    gate_values = jax.nn.sigmoid(
        jnp.einsum("rnd,dc->rnc", normed, proj_mats[4], preferred_element_type=jnp.float32)
    )
    pair_mid = pair_f + gate_values * update
    trans_in = (normalize(pair_mid, 2) * gain_vals[2]).astype(jnp.bfloat16).reshape(-1, channels)
    hidden = jax.nn.relu(jnp.dot(trans_in, up_mat, preferred_element_type=jnp.float32)).astype(
        jnp.bfloat16
    )
    pair_new = pair_mid + jnp.dot(hidden, down_mat, preferred_element_type=jnp.float32).reshape(
        pair_mid.shape
    )
    return pair_new.astype(jnp.bfloat16)


def per_device(pair_in, crop_mask, proj_weights, out_weights, up_weights, down_weights, norm_gains):
    section_index = lax.axis_index("section")
    section_count = lax.axis_size("section")
    micro_count = pair_in.shape[0]
    own_count = micro_count // section_count
    gathered = sent_together(
        (proj_weights, out_weights, up_weights, down_weights, norm_gains), "section", 0, 1
    )
    own_pairs = lax.dynamic_slice_in_dim(pair_in, section_index * own_count, own_count, 0)
    own_masks = lax.dynamic_slice_in_dim(crop_mask, section_index * own_count, own_count, 0).astype(
        jnp.float32
    )
    current = own_pairs[0]
    for layer_index in range(section_count):
        current = evo_block(
            current,
            own_masks[0],
            gathered[0][layer_index],
            gathered[1][layer_index],
            gathered[2][layer_index],
            gathered[3][layer_index],
            gathered[4][layer_index],
        )
    outputs = [current]
    return jnp.stack(outputs)


def solution(mesh):
    return jax.shard_map(
        per_device,
        mesh=mesh,
        in_specs=(
            P("groups", "axial", None, None),
            P("groups", None),
            P("section", None, None, None),
            P("section", None, None),
            P("section", None, None),
            P("section", None, None),
            P("section", None, None),
        ),
        out_specs=P(("groups", "section"), "axial", None, None),
        check_vma=False,
    )
```

profile of v0, /device:TPU:34, one launch (start us, length us, event | category | flops | bytes accessed | tf_op | source)
XLA Modules:
  0.0 615.9 jit_solution(15281660474628532459)
XLA Ops:
  14.7 61.3 %all-gather.3.cloned.1.call-done = bf16[4,1,229760]{2,1,0:T(2,128)(2,1)} async-done(((bf16[1,1,229760]{2,1,0:T(2,128)(2,1)}), bf16[4,1,229760]{2,1,0:T(2,128)(2,1)}) %all-gather.3.cloned.1.call-update) | async-done | bytes 1838096 | tf_op jit(solution)/shard_map/all_gather | solution.py:12
  76.0 3.9 copy.211
  80.5 11.9 %slice_reduce_fusion = (bf16[65536]{0:T(1024)(128)(2,1)}, bf16[65536]{0:T(1024)(128)(2,1)S(1)}, bf16[65536]{0:T(1024)(128)(2,1)S(1)}, bf16[65536]{0:T(1024)(128)...) fusion(bf16[4,229760]{1,0:T(4,128)(2,1)S(1)} %bitcast.338), kind=kLoop, calls=%fused_computation.231 | loop fusion | bytes 3145728 | tf_op jit(solution)/shard_map/slice | solution.py:96
  93.5 2.4 fusion.127
  95.9 1.9 slice_multiply_fusion.7
  99.3 2.6 reshape.477
  101.9 1.8 fusion.106
  103.7 46.5 %all_to_all.156 = bf16[32,4,8,256]{3,1,2,0:T(4,128)(2,1)S(1)} all-to-all(bf16[32,4,8,256]{3,1,2,0:T(4,128)(2,1)S(1)} %get-tuple-element.43), channel_id=1, replica_groups=mesh['groups'=2,'section'=4,'axial'=32] {'axial'}, dimensions={0} | all-to-all | bytes 1048576 | tf_op jit(solution)/shard_map/all_to_all | solution.py:51
  150.2 37.1 %all_to_all.157 = bf16[32,4,8,256]{3,1,2,0:T(4,128)(2,1)S(1)} all-to-all(bf16[32,4,8,256]{3,1,2,0:T(4,128)(2,1)S(1)} %get-tuple-element.44), channel_id=1, replica_groups=mesh['groups'=2,'section'=4,'axial'=32] {'axial'}, dimensions={0} | all-to-all | bytes 1048576 | tf_op jit(solution)/shard_map/all_to_all | solution.py:52
  188.8 4.8 all-to-all-start.2
  193.9 2.1 slice_reduce_fusion.13
  196.0 30.8 %all-to-all-done.2 = bf16[1,4,256,256]{3,1,0,2:T(4,128)(2,1)S(1)} async-done(((bf16[1,4,256,256]{3,1,0,2:T(4,128)(2,1)}), bf16[1,4,256,256]{3,1,0,2:T(4,128)(2,1)S(1)}, u32[]{:S(2)}, u32[]{:S(2)}) %all-to-all-start.2) | async-done | bytes 524320 | tf_op jit(solution)/shard_map/all_to_all | solution.py:55
  232.9 2.0 fusion.117
  234.9 1.6 slice_multiply_fusion.5
  236.8 1.5 reshape.479
  238.9 37.2 %all_to_all.158 = bf16[32,4,8,256]{3,1,2,0:T(4,128)(2,1)S(1)} all-to-all(bf16[32,4,8,256]{3,1,2,0:T(4,128)(2,1)S(1)} %get-tuple-element.41), channel_id=1, replica_groups=mesh['groups'=2,'section'=4,'axial'=32] {'axial'}, dimensions={0} | all-to-all | bytes 1048576 | tf_op jit(solution)/shard_map/all_to_all | solution.py:51
  276.1 37.1 %all_to_all.159 = bf16[32,4,8,256]{3,1,2,0:T(4,128)(2,1)S(1)} all-to-all(bf16[32,4,8,256]{3,1,2,0:T(4,128)(2,1)S(1)} %get-tuple-element.42), channel_id=1, replica_groups=mesh['groups'=2,'section'=4,'axial'=32] {'axial'}, dimensions={0} | all-to-all | bytes 1048576 | tf_op jit(solution)/shard_map/all_to_all | solution.py:52
  314.7 4.8 all-to-all-start.5
  319.9 32.8 %all-to-all-done.5 = bf16[1,4,256,256]{3,1,0,2:T(4,128)(2,1)S(1)} async-done(((bf16[1,4,256,256]{3,1,0,2:T(4,128)(2,1)}), bf16[1,4,256,256]{3,1,0,2:T(4,128)(2,1)S(1)}, u32[]{:S(2)}, u32[]{:S(2)}) %all-to-all-start.5) | async-done | bytes 524320 | tf_op jit(solution)/shard_map/all_to_all | solution.py:55
  358.1 2.0 fusion.115
  360.1 1.6 slice_multiply_fusion.3
  361.9 1.5 reshape.481
  364.1 37.1 %all_to_all.160 = bf16[32,4,8,256]{3,1,2,0:T(4,128)(2,1)S(1)} all-to-all(bf16[32,4,8,256]{3,1,2,0:T(4,128)(2,1)S(1)} %get-tuple-element.39), channel_id=1, replica_groups=mesh['groups'=2,'section'=4,'axial'=32] {'axial'}, dimensions={0} | all-to-all | bytes 1048576 | tf_op jit(solution)/shard_map/all_to_all | solution.py:51
  401.1 37.3 %all_to_all.161 = bf16[32,4,8,256]{3,1,2,0:T(4,128)(2,1)S(1)} all-to-all(bf16[32,4,8,256]{3,1,2,0:T(4,128)(2,1)S(1)} %get-tuple-element.40), channel_id=1, replica_groups=mesh['groups'=2,'section'=4,'axial'=32] {'axial'}, dimensions={0} | all-to-all | bytes 1048576 | tf_op jit(solution)/shard_map/all_to_all | solution.py:52
  440.0 4.8 all-to-all-start.8
  445.1 32.9 %all-to-all-done.8 = bf16[1,4,256,256]{3,1,0,2:T(4,128)(2,1)S(1)} async-done(((bf16[1,4,256,256]{3,1,0,2:T(4,128)(2,1)}), bf16[1,4,256,256]{3,1,0,2:T(4,128)(2,1)S(1)}, u32[]{:S(2)}, u32[]{:S(2)}) %all-to-all-start.8) | async-done | bytes 524320 | tf_op jit(solution)/shard_map/all_to_all | solution.py:55
  483.3 2.0 fusion.113
  485.3 1.6 slice_multiply_fusion.1
  489.2 37.1 %all_to_all.162 = bf16[32,4,8,256]{3,1,2,0:T(4,128)(2,1)S(1)} all-to-all(bf16[32,4,8,256]{3,1,2,0:T(4,128)(2,1)S(1)} %get-tuple-element.37), channel_id=1, replica_groups=mesh['groups'=2,'section'=4,'axial'=32] {'axial'}, dimensions={0} | all-to-all | bytes 1048576 | tf_op jit(solution)/shard_map/all_to_all | solution.py:51
  526.3 37.1 %all_to_all.163 = bf16[32,4,8,256]{3,1,2,0:T(4,128)(2,1)S(1)} all-to-all(bf16[32,4,8,256]{3,1,2,0:T(4,128)(2,1)S(1)} %get-tuple-element.38), channel_id=1, replica_groups=mesh['groups'=2,'section'=4,'axial'=32] {'axial'}, dimensions={0} | all-to-all | bytes 1048576 | tf_op jit(solution)/shard_map/all_to_all | solution.py:52
  564.9 5.1 all-to-all-start.11
  570.3 32.9 %all-to-all-done.11 = bf16[1,4,256,256]{3,1,0,2:T(4,128)(2,1)S(1)} async-done(((bf16[1,4,256,256]{3,1,0,2:T(4,128)(2,1)}), bf16[1,4,256,256]{3,1,0,2:T(4,128)(2,1)S(1)}, u32[]{:S(2)}, u32[]{:S(2)}) %all-to-all-start.11) | async-done | bytes 524320 | tf_op jit(solution)/shard_map/all_to_all | solution.py:55
  (163 shorter events, 44.6 us)
Async XLA Ops:
  6.5 6.4 %copy-start.1 = (bf16[4,8,256,128]{3,2,1,0:T(8,128)(2,1)S(1)}, bf16[4,8,256,128]{3,2,1,0:T(8,128)(2,1)}, u32[]{:S(2)}) copy-start(bf16[4,8,256,128]{3,2,1,0:T(8,128)(2,1)} %param.7) | copy-start | bytes 6291460
  6.5 69.4 %all-gather.3.cloned.1.call-start = ((), (), s32[]{:S(2)}) async-start(), calls=%async_computation.12 | async-start | bytes 4595200 | tf_op jit(solution)/shard_map/all_gather | solution.py:12
  11.9 0.9 copy-start
  13.9 0.6 copy-start.9
  14.7 78.8 %copy-start.12 = (f32[8,256]{1,0:T(8,128)}, f32[8,256]{1,0:T(8,128)S(1)}, u32[]{:S(2)}) copy-start(f32[8,256]{1,0:T(8,128)S(1)} %add_rsqrt_fusion.11) | copy-start | bytes 24580
  80.5 13.0 %copy-start.10 = (f32[8,256]{1,0:T(8,128)S(1)}, f32[8,256]{1,0:T(8,128)}, u32[]{:S(2)}) copy-start(f32[8,256]{1,0:T(8,128)} %copy-done.9) | copy-start | bytes 24580
  93.5 2.4 copy-start.24
  187.3 6.4 %copy-start.23 = (f32[128]{0:T(128)S(1)}, f32[128]{0:T(128)}, u32[]{:S(2)}) copy-start(f32[128]{0:T(128)} %get-tuple-element.75) | copy-start | bytes 1540
  187.3 6.6 %copy-start.4 = (bf16[65536]{0:T(1024)(128)(2,1)S(1)}, bf16[65536]{0:T(1024)(128)(2,1)}, u32[]{:S(2)}) copy-start(bf16[65536]{0:T(1024)(128)(2,1)} %get-tuple-element.15) | copy-start | bytes 393220
  188.8 38.0 %all-to-all-start.2 = ((bf16[1,4,256,256]{3,1,0,2:T(4,128)(2,1)}), bf16[1,4,256,256]{3,1,0,2:T(4,128)(2,1)S(1)}, u32[]{:S(2)}, u32[]{:S(2)}) async-start(bf16[1,4,256,256]{3,1,0,2:T(4,128)(2,1)} %copy.77), calls=%async_computation.2 | async-start | bytes 1048576 | tf_op jit(solution)/shard_map/all_to_all | solution.py:55
  226.9 1.6 copy-start.2
  227.0 1.6 copy-start.11
  227.0 1.6 copy-start.13
  227.0 1.6 copy-start.25
  228.5 1.6 copy-start.21
  230.1 1.3 copy-start.8
  231.5 1.5 copy-start.19
  313.2 6.4 %copy-start.22 = (f32[128]{0:T(128)S(1)}, f32[128]{0:T(128)}, u32[]{:S(2)}) copy-start(f32[128]{0:T(128)} %get-tuple-element.52) | copy-start | bytes 1540
  313.2 6.6 %copy-start.3 = (bf16[65536]{0:T(1024)(128)(2,1)S(1)}, bf16[65536]{0:T(1024)(128)(2,1)}, u32[]{:S(2)}) copy-start(bf16[65536]{0:T(1024)(128)(2,1)} %get-tuple-element.12) | copy-start | bytes 393220
  313.2 6.7 %copy-start.17 = (f32[1,384]{1,0:T(1,128)S(1)}, f32[1,384]{1,0:T(1,128)}, u32[]{:S(2)}) copy-start(f32[1,384]{1,0:T(1,128)} %get-tuple-element.34) | copy-start | bytes 4612
  314.7 38.0 %all-to-all-start.5 = ((bf16[1,4,256,256]{3,1,0,2:T(4,128)(2,1)}), bf16[1,4,256,256]{3,1,0,2:T(4,128)(2,1)S(1)}, u32[]{:S(2)}, u32[]{:S(2)}) async-start(bf16[1,4,256,256]{3,1,0,2:T(4,128)(2,1)} %copy.87), calls=%async_computation.5 | async-start | bytes 1048576 | tf_op jit(solution)/shard_map/all_to_all | solution.py:55
  352.9 0.8 copy-start.16
  352.9 0.8 copy-start.20
  353.7 1.6 copy-start.18
  355.3 1.3 copy-start.7
  440.0 38.0 %all-to-all-start.8 = ((bf16[1,4,256,256]{3,1,0,2:T(4,128)(2,1)}), bf16[1,4,256,256]{3,1,0,2:T(4,128)(2,1)S(1)}, u32[]{:S(2)}, u32[]{:S(2)}) async-start(bf16[1,4,256,256]{3,1,0,2:T(4,128)(2,1)} %copy.97), calls=%async_computation.8 | async-start | bytes 1048576 | tf_op jit(solution)/shard_map/all_to_all | solution.py:55
  478.1 0.8 copy-start.15
  480.5 1.3 copy-start.6
  564.9 38.2 %all-to-all-start.11 = ((bf16[1,4,256,256]{3,1,0,2:T(4,128)(2,1)}), bf16[1,4,256,256]{3,1,0,2:T(4,128)(2,1)S(1)}, u32[]{:S(2)}, u32[]{:S(2)}) async-start(bf16[1,4,256,256]{3,1,0,2:T(4,128)(2,1)} %copy.107), calls=%async_computation.11 | async-start | bytes 1048576 | tf_op jit(solution)/shard_map/all_to_all | solution.py:55
  603.3 0.8 copy-start.14
  605.7 1.3 copy-start.5
Sparse Core Ops, SparseCore 0:
  13.0 62.9 all-gather.2
where the time goes:
time: 627 us; the launch traced here: 616 us
  blocking collectives  306 us (49%)
  waiting for transfers between devices  191 us (30%)
  local copies, waits for them, and re-layouts  41.9 us (7%)
  other arithmetic  21.5 us (3%)
  matrix products  21.3 us (3%)
  starting transfers between devices  19.5 us (3%)
  between operations  14.6 us (2%)
    all_to_all x4, blocking collectives, evo_block(): lax.all_to_all(left_groups, 'axial', split_axis=0, concat_axis=2, tiled=T...  158 us
    all_to_all x4, blocking collectives, evo_block(): lax.all_to_all(right_groups, 'axial', split_axis=0, concat_axis=2, tiled=...  148 us
    all_to_all x4, waiting for transfers between devices, evo_block(): lax.all_to_all(product, 'axial', split_axis=2, concat_axis=0, tiled=True)  129 us
    all_gather x1, waiting for transfers between devices, sent_together(): result, at, outs = (lax.all_gather(both, axis, axis=dim, tiled=True), 0, [])  61.3 us
    all_to_all x4, starting transfers between devices, evo_block(): lax.all_to_all(product, 'axial', split_axis=2, concat_axis=0, tiled=True)  19.5 us
  transfers between devices with their start and end apart: 5, of which 5 were waited for; matrix products, arithmetic and copies ran while one was open for 1% of the time, Pallas kernels for 0%

commit v1 on v0

v1 whole, which is shorter than its diff:
```python
import functools

import jax
import jax.numpy as jnp
from jax import lax
from jax.experimental import pallas as pl
from jax.experimental.pallas import tpu as pltpu
from jax.sharding import PartitionSpec as P

EPS = 1e-05
MESH = pl.DeviceIdType.MESH
F32 = jnp.float32
BF16 = jnp.bfloat16
LANES = 128
SUB = 8


def sigmoid(v):
    return 0.5 * jnp.tanh(0.5 * v) + 0.5


def norm_rows(v):
    center = v - jnp.mean(v, axis=0, keepdims=True)
    spread = jnp.mean(center * center, axis=0, keepdims=True)
    return center * lax.rsqrt(spread + EPS)


def mm(a, b):
    return jnp.dot(a, b, preferred_element_type=F32)


def kernel(
    S, G, R, C, FF, blocks,
    pair_ref, mask_ref, proj_ref, wout_ref, up_ref, down_ref, gain_ref,
    out_ref,
    XB, ZIN, ZT, NB, GATE, SB, LB, TB, OB, S2L, S2R, S3, RS, PM, ZO, YA, YB,
    WP, WO, WU, WD, GN, WPT, WOT, WUT, WDT, GC,
    in_send, in_recv, out_send, out_recv,
    xb_send, xb_recv, z_send, z_recv,
    ya_send, ya_recv, yb_send, yb_recv, o_send, o_recv,
    w_send, w_recv,
):
    M = S * G
    E = R // S
    CPO = C // M
    x = lax.axis_index("section")
    A = lax.axis_index("axial")
    m = lax.div(A, G)
    t = lax.rem(A, G)
    a = x * G + t

    def wrap(v, n):
        return lax.rem(v + 2 * n, n)

    def member(d):
        return {"section": lax.div(d, G), "axial": m * G + lax.rem(d, G)}

    def along_z(seg):
        return {"section": x, "axial": seg * G + t}

    def along_x(sec):
        return {"section": sec, "axial": A}

    def remote(src, dst, ss, rs, dev):
        return pltpu.make_async_remote_copy(
            src_ref=src, dst_ref=dst, send_sem=ss, recv_sem=rs,
            device_id=dev, device_id_type=MESH,
        )

    barrier = pltpu.get_barrier_semaphore()

    def greet(k, c):
        pl.semaphore_signal(
            barrier, inc=1, device_id=member(lax.rem(a + k, M)), device_id_type=MESH
        )
        return c

    lax.fori_loop(1, M, greet, 0)
    for k in range(1, S):
        pl.semaphore_signal(
            barrier, inc=1, device_id=along_z(wrap(m + k, S)), device_id_type=MESH
        )
    pl.semaphore_wait(barrier, M - 1 + S - 1)

    def xb_copy(k, h):
        dest = wrap(m + k, S)
        return remote(
            pair_ref.at[dest, pl.ds(E * x, E), pl.ds(h * LANES, LANES), :],
            XB.at[m, h],
            xb_send.at[k, h], xb_recv.at[k, h], along_z(dest),
        )

    def xb_local(h):
        return pltpu.make_async_copy(
            pair_ref.at[m, pl.ds(E * x, E), pl.ds(h * LANES, LANES), :],
            XB.at[m, h], xb_recv.at[0, h],
        )

    weights = ((proj_ref, WP), (wout_ref, WO), (up_ref, WU), (down_ref, WD), (gain_ref, GN))

    def w_copy(k, i):
        src, dst = weights[i]
        return remote(
            src.at[0], dst.at[x], w_send.at[k, i], w_recv.at[k, i], along_x(wrap(x + k, S))
        )

    def w_local(i):
        src, dst = weights[i]
        return pltpu.make_async_copy(src.at[0], dst.at[x], w_recv.at[0, i])

    order = (S // 2,) + tuple(k for k in range(1, S) if k != S // 2)
    for h in range(2):
        for k in order:
            xb_copy(k, h).start()
        xb_local(h).start()
    for i in range(len(weights)):
        w_local(i).start()
        for k in range(1, S):
            w_copy(k, i).start()

    q = mask_ref[pl.ds(m, 1), :].astype(F32)
    n_res = q.shape[1]
    lane = lax.broadcasted_iota(jnp.int32, (R, n_res), 1)
    row = lax.broadcasted_iota(jnp.int32, (R, n_res), 0) + a * R
    q_rows = jnp.sum(jnp.where(lane == row, q, 0.0), axis=1, keepdims=True)
    pair_mask = q_rows * q
    for h in range(2):
        PM[h] = pair_mask[:, h * LANES : (h + 1) * LANES]

    for i in range(len(weights)):
        w_local(i).wait()
        for k in range(1, S):
            w_copy(k, i).wait_recv()

    def flip(v):
        return v.astype(F32).T.astype(BF16)

    def flip_weights(l, c):
        for e in range(5):
            WPT[l, e * C : (e + 1) * C, :] = flip(WP[l, e])
        WOT[l] = flip(WO[l])
        for f in range(FF // C):
            WUT[l, f * C : (f + 1) * C, :] = flip(WU[l, :, f * C : (f + 1) * C])
            WDT[l, :, f * C : (f + 1) * C] = flip(WD[l, f * C : (f + 1) * C, :])
        for g in range(3):
            GC[l, g] = jnp.broadcast_to(GN[l, g : g + 1, :], (LANES, C)).T
        return c

    lax.fori_loop(0, blocks, flip_weights, 0)

    def z_copy(k, h):
        sec = wrap(x + k, S)
        return remote(
            XB.at[sec, h], ZIN.at[h, pl.ds(E * x, E)],
            z_send.at[k, h], z_recv.at[k, h], along_x(sec),
        )

    def forward(h):
        for k in order + (0,):
            sec = wrap(x + k, S)
            kz = wrap(m - sec, S)
            pltpu.make_async_copy(XB.at[sec, h], XB.at[sec, h], xb_recv.at[kz, h]).wait()
            if k:
                z_copy(k, h).start()
            else:
                ZIN[h, pl.ds(E * x, E)] = XB[x, h]

    def gather_in(h):
        for k in range(1, S):
            z_copy(k, h).wait_recv()

        def turn(rp, c):
            parts = [ZIN[h, 2 * rp + e].astype(F32).T for e in range(2)]
            ZT[h, rp] = jnp.concatenate(parts, axis=1).astype(BF16)
            return c

        lax.fori_loop(0, R // 2, turn, 0)

    def wide(v):
        return jnp.concatenate([v, v], axis=1)

    def in_copy(h, d):
        return remote(
            SB.at[h, d], LB.at[h, a], in_send.at[h], in_recv.at[h], member(d)
        )

    def in_all(h):
        return remote(
            SB.at[h, pl.ds(0, M - 1)], LB.at[h, pl.ds(0, M - 1)],
            in_send.at[h], in_recv.at[h], member(lax.rem(a + 1, M)),
        )

    def out_copy(h, d):
        return remote(
            TB.at[h, d], OB.at[h, a], out_send.at[h], out_recv.at[h], member(d)
        )

    def out_all(h):
        return remote(
            TB.at[h, pl.ds(0, M - 1)], OB.at[h, pl.ds(0, M - 1)],
            out_send.at[h], out_recv.at[h], member(lax.rem(a + 1, M)),
        )

    def start_all(copy, h):
        def go(k, c):
            copy(h, lax.rem(a + k, M)).start()
            return c

        lax.fori_loop(1, M, go, 0)

    def pre(l, h):
        g0 = wide(GC[l, 0])

        def project(rp, c):
            normed = (norm_rows(ZT[h, rp].astype(F32)) * g0).astype(BF16)
            NB[h, rp] = normed
            lin = mm(WPT[l, 0 : 4 * C, :], normed)
            pm = jnp.concatenate([PM[h, pl.ds(2 * rp, 1), :], PM[h, pl.ds(2 * rp + 1, 1), :]], axis=1)
            left = sigmoid(lin[C : 2 * C]) * lin[0:C] * pm
            right = sigmoid(lin[3 * C : 4 * C]) * lin[2 * C : 3 * C] * pm
            for e in range(2):
                rows = pl.ds(2 * rp + e, C, stride=SUB)
                S2L[rows, :] = left[:, e * LANES : (e + 1) * LANES]
                S2R[rows, :] = right[:, e * LANES : (e + 1) * LANES]
            return c

        lax.fori_loop(0, R // 2, project, 0)

        @pl.when(l > 0)
        def _():
            in_all(h).wait_send()

        SB[h, :, 0] = S2L[...].reshape(M, CPO, SUB, LANES).astype(BF16)
        SB[h, :, 1] = S2R[...].reshape(M, CPO, SUB, LANES).astype(BF16)
        start_all(in_copy, h)
        LB[h, a] = SB[h, a]

        def gates(rp, c):
            GATE[h, rp] = sigmoid(mm(WPT[l, 4 * C : 5 * C, :], NB[h, rp]))
            return c

        lax.fori_loop(0, R // 2, gates, 0)

    def triangle(l):
        for h in range(2):
            in_all(h).wait_recv()

        @pl.when(l > 0)
        def _():
            for h in range(2):
                out_all(h).wait_send()

        def channel(c, carry):
            def side(lr):
                halves = [
                    LB[h, :, lr, c].astype(F32).reshape(M * SUB, LANES).astype(BF16)
                    for h in range(2)
                ]
                return jnp.concatenate(halves, axis=1)

            prod = lax.dot_general(
                side(0), side(1), (((1,), (1,)), ((), ())), preferred_element_type=F32
            )
            for h in range(2):
                TB[h, :, c] = (
                    prod[:, h * LANES : (h + 1) * LANES].reshape(M, SUB, LANES).astype(BF16)
                )
            return carry

        lax.fori_loop(0, CPO, channel, 0)
        for h in range(2):
            start_all(out_copy, h)
        for h in range(2):
            OB[h, a] = TB[h, a]

    def post(l, h):
        out_all(h).wait_recv()
        got = OB[h].astype(F32).reshape(C, SUB, LANES)
        mean = jnp.sum(got, axis=0) * (1.0 / C)
        center = got - mean[None]
        S3[...] = center.reshape(C * SUB, LANES)
        RS[...] = lax.rsqrt(jnp.sum(center * center, axis=0) * (1.0 / C) + EPS)
        g1 = wide(GC[l, 1])
        g2 = wide(GC[l, 2])

        def update(rp, c):
            vals = jnp.concatenate(
                [S3[pl.ds(2 * rp + e, C, stride=SUB), :] for e in range(2)], axis=1
            )
            scale = jnp.concatenate([RS[pl.ds(2 * rp + e, 1), :] for e in range(2)], axis=1)
            tri_norm = (vals * scale * g1).astype(BF16)
            mid = ZT[h, rp].astype(F32) + GATE[h, rp] * mm(WOT[l], tri_norm)
            trans_in = (norm_rows(mid) * g2).astype(BF16)
            hidden = jnp.maximum(mm(WUT[l], trans_in), 0.0).astype(BF16)
            ZT[h, rp] = (mid + mm(WDT[l], hidden)).astype(BF16)
            return c

        lax.fori_loop(0, R // 2, update, 0)

    for h in range(2):
        forward(h)
    for h in range(2):
        gather_in(h)
        pre(0, h)

    def block(l, c):
        triangle(l)
        for h in range(2):
            post(l, h)

            @pl.when(l < blocks - 1)
            def _():
                pre(l + 1, h)

        return c

    lax.fori_loop(0, blocks, block, 0)

    def ya_copy(k, h):
        sec = wrap(x + k, S)
        return remote(
            ZO.at[h, pl.ds(E * sec, E)], YA.at[x, h],
            ya_send.at[k, h], ya_recv.at[k, h], along_x(sec),
        )

    def yb_copy(k, h):
        seg = wrap(m + k, S)
        return remote(
            YA.at[seg, h], YB.at[m, h], yb_send.at[k, h], yb_recv.at[k, h], along_z(seg)
        )

    def o_slice(h):
        return out_ref.at[0, pl.ds(E * x, E), pl.ds(h * LANES, LANES), :]

    def o_copy(k, h):
        sec = wrap(x + k, S)
        return remote(
            YB.at[sec, h], o_slice(h), o_send.at[k, h], o_recv.at[k, h], along_x(sec)
        )

    def o_local(h):
        return pltpu.make_async_copy(YB.at[x, h], o_slice(h), o_recv.at[0, h])

    for h in range(2):
        def turn_back(rp, c, h=h):
            v = ZT[h, rp].astype(F32)
            for e in range(2):
                ZO[h, 2 * rp + e] = v[:, e * LANES : (e + 1) * LANES].T.astype(BF16)
            return c

        lax.fori_loop(0, R // 2, turn_back, 0)
        for k in order:
            ya_copy(k, h).start()
        YA[x, h] = ZO[h, pl.ds(E * x, E)]
    for h in range(2):
        for k in order + (0,):
            seg = wrap(m + k, S)
            kx = wrap(x - seg, S)

            @pl.when(kx != 0)
            def _():
                pltpu.make_async_copy(YA.at[seg, h], YA.at[seg, h], ya_recv.at[kx, h]).wait()

            if k:
                yb_copy(k, h).start()
            else:
                YB[m, h] = YA[m, h]
    for h in range(2):
        for k in order + (0,):
            sec = wrap(x + k, S)
            kz = wrap(m - sec, S)

            @pl.when(kz != 0)
            def _():
                pltpu.make_async_copy(YB.at[sec, h], YB.at[sec, h], yb_recv.at[kz, h]).wait()

            if k:
                o_copy(k, h).start()
            else:
                o_local(h).start()
    for h in range(2):
        in_all(h).wait_send()
        out_all(h).wait_send()
        o_local(h).wait()
        for k in range(1, S):
            xb_copy(k, h).wait_send()
            z_copy(k, h).wait_send()
            ya_copy(k, h).wait_send()
            yb_copy(k, h).wait_send()
            o_copy(k, h).wait_send()
            o_copy(k, h).wait_recv()
    for i in range(len(weights)):
        for k in range(1, S):
            w_copy(k, i).wait_send()


def per_device(pair_in, crop_mask, proj_weights, out_weights, up_weights, down_weights, norm_gains):
    S = lax.axis_size("section")
    G = lax.axis_size("axial") // S
    MB, R, N, C = pair_in.shape
    FF = up_weights.shape[-1]
    M = S * G
    CPO = C // M
    E = R // S
    assert MB == S and R == SUB and N == 2 * LANES and C == LANES and N == R * M
    gains = jnp.pad(norm_gains.astype(F32), ((0, 0), (0, SUB - norm_gains.shape[1]), (0, 0)))
    any_spec = pl.BlockSpec(memory_space=pl.ANY)
    vmem_spec = pl.BlockSpec(memory_space=pltpu.VMEM)
    V = pltpu.VMEM
    dma = pltpu.SemaphoreType.DMA
    return pl.pallas_call(
        functools.partial(kernel, S, G, R, C, FF, S),
        out_shape=jax.ShapeDtypeStruct((1, R, N, C), BF16),
        in_specs=[any_spec, vmem_spec] + [any_spec] * 5,
        out_specs=any_spec,
        scratch_shapes=[
            V((S, 2, E, LANES, C), BF16),
            V((2, R, LANES, C), BF16),
            V((2, R // 2, C, 2 * LANES), BF16),
            V((2, R // 2, C, 2 * LANES), BF16),
            V((2, R // 2, C, 2 * LANES), F32),
            V((2, M, 2, CPO, SUB, LANES), BF16),
            V((2, M, 2, CPO, SUB, LANES), BF16),
            V((2, M, CPO, SUB, LANES), BF16),
            V((2, M, CPO, SUB, LANES), BF16),
            V((C * SUB, LANES), F32),
            V((C * SUB, LANES), F32),
            V((C * SUB, LANES), F32),
            V((SUB, LANES), F32),
            V((2, SUB, LANES), F32),
            V((2, R, LANES, C), BF16),
            V((S, 2, E, LANES, C), BF16),
            V((S, 2, E, LANES, C), BF16),
            V((S, 5, C, C), BF16),
            V((S, C, C), BF16),
            V((S, C, FF), BF16),
            V((S, FF, C), BF16),
            V((S, SUB, C), F32),
            V((S, 5 * C, C), BF16),
            V((S, C, C), BF16),
            V((S, FF, C), BF16),
            V((S, C, FF), BF16),
            V((S, 3, C, LANES), F32),
        ]
        + [dma((2,))] * 4
        + [dma((S, 2))] * 10
        + [dma((S, 5))] * 2,
        compiler_params=pltpu.CompilerParams(
            collective_id=0, has_side_effects=True, vmem_limit_bytes=56 * 1024 * 1024
        ),
    )(pair_in, crop_mask, proj_weights, out_weights, up_weights, down_weights, gains)


def solution(mesh):
    return jax.shard_map(
        per_device,
        mesh=mesh,
        in_specs=(
            P("groups", "axial", None, None),
            P("groups", None),
            P("section", None, None, None),
            P("section", None, None),
            P("section", None, None),
            P("section", None, None),
            P("section", None, None),
        ),
        out_specs=P(("groups", "section"), "axial", None, None),
        check_vma=False,
    )
```

time: 627 us -> 251 us (0.40); the launches traced: 616 us -> 248 us
  blocking collectives: 306 us -> 0 us
  Pallas kernels: 0 us -> 245 us
  waiting for transfers between devices: 191 us -> 0 us
  local copies, waits for them, and re-layouts: 41.9 us -> 1.87 us
  matrix products: 21.3 us -> 0 us
  other arithmetic: 21.5 us -> 1.27 us
  starting transfers between devices: 19.5 us -> 0 us
  between operations: 14.6 us -> 0.01 us
    all_to_all x8 -> x0, blocking collectives: 306 us -> none  [the longest x4 158 us: evo_block(): lax.all_to_all(left_groups, 'axial', split_axis=0, concat_axis=2, tiled=T...]
    pallas_call x0 -> x1, Pallas kernels: none -> 245 us  [per_device(): pl.pallas_call(functools.partial(kernel, S, G, R, C, FF, S), out_shape=ja...]
    all_to_all x4 -> x0, waiting for transfers between devices: 129 us -> none  [evo_block(): lax.all_to_all(product, 'axial', split_axis=2, concat_axis=0, tiled=True)]
    all_gather x1 -> x0, waiting for transfers between devices: 61.3 us -> none  [sent_together(): result, at, outs = (lax.all_gather(both, axis, axis=dim, tiled=True), 0, [])]
    dot_general x24 -> x0, matrix products: 21.3 us -> none  [the longest x4 8.26 us: evo_block(): jnp.einsum('rnd,edc->ecrn', normed, proj_mats[:4], preferred_element_type...]
    all_to_all x4 -> x0, starting transfers between devices: 19.5 us -> none  [evo_block(): lax.all_to_all(product, 'axial', split_axis=2, concat_axis=0, tiled=True)]
    slice x2 -> x0, local copies, waits for them, and re-layouts: 14 us -> none  [the longest x1 11.9 us: per_device(): gathered[3][layer_index]]
    mul x19 -> x0, local copies, waits for them, and re-layouts: 11.5 us -> none  [the longest x4 7.15 us: evo_block(): jax.nn.sigmoid(linear[3]) * linear[2] * pair_mask]
  transfers between devices with their start and end apart: 5 -> 0, of which waited for: 5 -> 0; matrix products, arithmetic and copies ran while one was open for 1% -> 0% of each run, Pallas kernels for 0% -> 0%
where the time goes in v1:
time: 251 us; the launch traced here: 248 us
  Pallas kernels  245 us (98%)
    pallas_call x1, Pallas kernels, per_device(): pl.pallas_call(functools.partial(kernel, S, G, R, C, FF, S), out_shape=ja...  245 us

profile of v1, /device:TPU:34, one launch (start us, length us, event | category | flops | bytes accessed | tf_op | source)
XLA Modules:
  0.0 248.3 jit_solution(7709521733713739430)
XLA Ops:
  0.0 1.3 pad_convert_fusion.gain_ref
  1.3 245.1 %shard_map.73 = bf16[1,8,256,128]{3,2,1,0:T(8,128)(2,1)} custom-call(bf16[4,8,256,128]{3,2,1,0:T(8,128)(2,1)} %pair_ref.1, s32[4,256]{1,0:T(4,128)} %mask_ref.1, bf16[1,5,128,128]{3,2,1,0:T(8,128)(2,1)} %proj_ref.1, bf16[1,128,128]{2,1,0:T(8,128)(2,1)} %wout_ref.1, bf16[1,128,512]{2,1,0:T(8,128)(2,1)} %up_ref.1, bf16[1,512,128]{2,1,0:T(8,128)(2,1)} %down_ref.1, ...), custom_call_target="tpu_custom_call" | custom-call | tf_op jit(solution)/shard_map/pallas_call | solution.py:411
  246.4 1.9 copy.9

commit v2 on v1

--- a/solution.py
+++ b/solution.py
@@ -108,15 +108,28 @@
         src, dst = weights[i]
         return pltpu.make_async_copy(src.at[0], dst.at[x], w_recv.at[0, i])
 
+    def w_send_all(l, which):
+        @pl.when(x == l)
+        def _():
+            for i in which:
+                for k in range(1, S):
+                    w_copy(k, i).start()
+
+    def w_arrived(l, which):
+        k = wrap(x - l, S)
+        for i in which:
+            dst = weights[i][1]
+            pltpu.make_async_copy(dst.at[l], dst.at[l], w_recv.at[k, i]).wait()
+
+    early, late = (0, 4), (1, 2, 3)
     order = (S // 2,) + tuple(k for k in range(1, S) if k != S // 2)
     for h in range(2):
         for k in order:
             xb_copy(k, h).start()
         xb_local(h).start()
-    for i in range(len(weights)):
+    for i in early + late:
         w_local(i).start()
-        for k in range(1, S):
-            w_copy(k, i).start()
+    w_send_all(0, early)
 
     q = mask_ref[pl.ds(m, 1), :].astype(F32)
     n_res = q.shape[1]
@@ -127,26 +140,22 @@
     for h in range(2):
         PM[h] = pair_mask[:, h * LANES : (h + 1) * LANES]
 
-    for i in range(len(weights)):
-        w_local(i).wait()
-        for k in range(1, S):
-            w_copy(k, i).wait_recv()
-
     def flip(v):
         return v.astype(F32).T.astype(BF16)
 
-    def flip_weights(l, c):
+    def flip_early(l):
+        w_arrived(l, early)
         for e in range(5):
             WPT[l, e * C : (e + 1) * C, :] = flip(WP[l, e])
+        for g in range(3):
+            GC[l, g] = jnp.broadcast_to(GN[l, g : g + 1, :].astype(F32), (LANES, C)).T
+
+    def flip_late(l):
+        w_arrived(l, late)
         WOT[l] = flip(WO[l])
         for f in range(FF // C):
             WUT[l, f * C : (f + 1) * C, :] = flip(WU[l, :, f * C : (f + 1) * C])
             WDT[l, :, f * C : (f + 1) * C] = flip(WD[l, f * C : (f + 1) * C, :])
-        for g in range(3):
-            GC[l, g] = jnp.broadcast_to(GN[l, g : g + 1, :], (LANES, C)).T
-        return c
-
-    lax.fori_loop(0, blocks, flip_weights, 0)
 
     def z_copy(k, h):
         sec = wrap(x + k, S)
@@ -297,25 +306,6 @@
 
         lax.fori_loop(0, R // 2, update, 0)
 
-    for h in range(2):
-        forward(h)
-    for h in range(2):
-        gather_in(h)
-        pre(0, h)
-
-    def block(l, c):
-        triangle(l)
-        for h in range(2):
-            post(l, h)
-
-            @pl.when(l < blocks - 1)
-            def _():
-                pre(l + 1, h)
-
-        return c
-
-    lax.fori_loop(0, blocks, block, 0)
-
     def ya_copy(k, h):
         sec = wrap(x + k, S)
         return remote(
@@ -341,8 +331,8 @@
     def o_local(h):
         return pltpu.make_async_copy(YB.at[x, h], o_slice(h), o_recv.at[0, h])
 
-    for h in range(2):
-        def turn_back(rp, c, h=h):
+    def spread(h):
+        def turn_back(rp, c):
             v = ZT[h, rp].astype(F32)
             for e in range(2):
                 ZO[h, 2 * rp + e] = v[:, e * LANES : (e + 1) * LANES].T.astype(BF16)
@@ -352,6 +342,43 @@
         for k in order:
             ya_copy(k, h).start()
         YA[x, h] = ZO[h, pl.ds(E * x, E)]
+
+    forward(0)
+    flip_early(0)
+    gather_in(0)
+    pre(0, 0)
+    forward(1)
+    w_send_all(0, late)
+    w_send_all(1, early + late)
+    gather_in(1)
+    pre(0, 1)
+
+    def block(l, c):
+        @pl.when(l < blocks - 2)
+        def _():
+            w_send_all(l + 2, early + late)
+
+        flip_late(l)
+
+        @pl.when(l < blocks - 1)
+        def _():
+            flip_early(l + 1)
+
+        triangle(l)
+        for h in range(2):
+            post(l, h)
+
+            @pl.when(l < blocks - 1)
+            def _():
+                pre(l + 1, h)
+
+            @pl.when(l == blocks - 1)
+            def _():
+                spread(h)
+
+        return c
+
+    lax.fori_loop(0, blocks, block, 0)
     for h in range(2):
         for k in order + (0,):
             seg = wrap(m + k, S)
@@ -403,7 +430,6 @@
     CPO = C // M
     E = R // S
     assert MB == S and R == SUB and N == 2 * LANES and C == LANES and N == R * M
-    gains = jnp.pad(norm_gains.astype(F32), ((0, 0), (0, SUB - norm_gains.shape[1]), (0, 0)))
     any_spec = pl.BlockSpec(memory_space=pl.ANY)
     vmem_spec = pl.BlockSpec(memory_space=pltpu.VMEM)
     V = pltpu.VMEM
@@ -435,7 +461,7 @@
             V((S, C, C), BF16),
             V((S, C, FF), BF16),
             V((S, FF, C), BF16),
-            V((S, SUB, C), F32),
+            V((S, 3, C), BF16),
             V((S, 5 * C, C), BF16),
             V((S, C, C), BF16),
             V((S, FF, C), BF16),
@@ -448,7 +474,7 @@
         compiler_params=pltpu.CompilerParams(
             collective_id=0, has_side_effects=True, vmem_limit_bytes=56 * 1024 * 1024
         ),
-    )(pair_in, crop_mask, proj_weights, out_weights, up_weights, down_weights, gains)
+    )(pair_in, crop_mask, proj_weights, out_weights, up_weights, down_weights, norm_gains)
 
 
 def solution(mesh):

time: 251 us -> 275 us (1.096)
  Pallas kernels: 245 us -> 269 us
    pallas_call x1, Pallas kernels: 245 us -> 269 us  [per_device(): pl.pallas_call(functools.partial(kernel, S, G, R, C, FF, S), out_shape=ja...]
where the time goes in v2:
time: 275 us; the launch traced here: 271 us
  Pallas kernels  269 us (98%)
    pallas_call x1, Pallas kernels, per_device(): pl.pallas_call(functools.partial(kernel, S, G, R, C, FF, S), out_shape=ja...  269 us

profile of v2, /device:TPU:34, one launch (start us, length us, event | category | flops | bytes accessed | tf_op | source)
XLA Modules:
  0.0 271.0 jit_solution(11760813001300841276)
XLA Ops:
  0.0 269.1 %shard_map.73 = bf16[1,8,256,128]{3,2,1,0:T(8,128)(2,1)} custom-call(bf16[4,8,256,128]{3,2,1,0:T(8,128)(2,1)} %pair_ref.1, s32[4,256]{1,0:T(4,128)} %mask_ref.1, bf16[1,5,128,128]{3,2,1,0:T(8,128)(2,1)} %proj_ref.1, bf16[1,128,128]{2,1,0:T(8,128)(2,1)} %wout_ref.1, bf16[1,128,512]{2,1,0:T(8,128)(2,1)} %up_ref.1, bf16[1,512,128]{2,1,0:T(8,128)(2,1)} %down_ref.1, ...), custom_call_target="tpu_custom_call" | custom-call | tf_op jit(solution)/shard_map/pallas_call | solution.py:437
  269.1 1.9 copy.9

commit v3 on v2

--- a/solution.py
+++ b/solution.py
@@ -33,27 +33,34 @@
     S, G, R, C, FF, blocks,
     pair_ref, mask_ref, proj_ref, wout_ref, up_ref, down_ref, gain_ref,
     out_ref,
-    XB, ZIN, ZT, NB, GATE, SB, LB, TB, OB, S2L, S2R, S3, RS, PM, ZO, YA, YB,
+    XB, ZIN, ZT, NB, GATE, SB, LL, RR, TB, OB, S2L, S2R, S3, RS, PM, ZO, YA, YB,
     WP, WO, WU, WD, GN, WPT, WOT, WUT, WDT, GC,
-    in_send, in_recv, out_send, out_recv,
+    l_send, l_recv, i_send, out_send, out_recv, i_recv,
     xb_send, xb_recv, z_send, z_recv,
     ya_send, ya_recv, yb_send, yb_recv, o_send, o_recv,
-    w_send, w_recv,
+    w_send, w_recv, r_send, r_recv,
 ):
     M = S * G
+    GH = G // 2
+    MH = M // 2
     E = R // S
-    CPO = C // M
+    CPO = C // MH
     x = lax.axis_index("section")
     A = lax.axis_index("axial")
     m = lax.div(A, G)
     t = lax.rem(A, G)
     a = x * G + t
+    half = lax.div(t, GH)
+    mine = x * GH + lax.rem(t, GH)
 
     def wrap(v, n):
         return lax.rem(v + 2 * n, n)
 
     def member(d):
         return {"section": lax.div(d, G), "axial": m * G + lax.rem(d, G)}
+
+    def in_half(hf, i):
+        return {"section": lax.div(i, GH), "axial": m * G + hf * GH + lax.rem(i, GH)}
 
     def along_z(seg):
         return {"section": x, "axial": seg * G + t}
@@ -108,18 +115,37 @@
         src, dst = weights[i]
         return pltpu.make_async_copy(src.at[0], dst.at[x], w_recv.at[0, i])
 
-    def w_send_all(l, which):
-        @pl.when(x == l)
-        def _():
-            for i in which:
-                for k in range(1, S):
-                    w_copy(k, i).start()
-
-    def w_arrived(l, which):
+    core = lax.rem(A, 2)
+    sibling = A + 1 - 2 * core
+
+    def w_relay_copy(l, i):
+        dst = weights[i][1]
+        return remote(
+            dst.at[l], dst.at[l], r_send.at[l, i], r_recv.at[l, i],
+            {"section": x, "axial": sibling},
+        )
+
+    def w_relay(l):
         k = wrap(x - l, S)
+        for turn, which in ((0, early), (1, late)):
+            @pl.when((x != l) & (core == turn))
+            def _():
+                for i in which:
+                    dst = weights[i][1]
+                    pltpu.make_async_copy(dst.at[l], dst.at[l], w_recv.at[k, i]).wait()
+                    w_relay_copy(l, i).start()
+
+    def w_arrived(l, which, turn):
         for i in which:
             dst = weights[i][1]
-            pltpu.make_async_copy(dst.at[l], dst.at[l], w_recv.at[k, i]).wait()
+
+            @pl.when(x == l)
+            def _():
+                pltpu.make_async_copy(dst.at[l], dst.at[l], w_recv.at[0, i]).wait()
+
+            @pl.when((x != l) & (core != turn))
+            def _():
+                w_relay_copy(l, i).wait_recv()
 
     early, late = (0, 4), (1, 2, 3)
     order = (S // 2,) + tuple(k for k in range(1, S) if k != S // 2)
@@ -129,7 +155,12 @@
         xb_local(h).start()
     for i in early + late:
         w_local(i).start()
-    w_send_all(0, early)
+    for turn, which in ((0, early), (1, late)):
+        @pl.when(core == turn)
+        def _():
+            for i in which:
+                for k in order:
+                    w_copy(k, i).start()
 
     q = mask_ref[pl.ds(m, 1), :].astype(F32)
     n_res = q.shape[1]
@@ -144,14 +175,14 @@
         return v.astype(F32).T.astype(BF16)
 
     def flip_early(l):
-        w_arrived(l, early)
+        w_arrived(l, early, 0)
         for e in range(5):
             WPT[l, e * C : (e + 1) * C, :] = flip(WP[l, e])
         for g in range(3):
             GC[l, g] = jnp.broadcast_to(GN[l, g : g + 1, :].astype(F32), (LANES, C)).T
 
     def flip_late(l):
-        w_arrived(l, late)
+        w_arrived(l, late, 1)
         WOT[l] = flip(WO[l])
         for f in range(FF // C):
             WUT[l, f * C : (f + 1) * C, :] = flip(WU[l, :, f * C : (f + 1) * C])
@@ -188,34 +219,66 @@
     def wide(v):
         return jnp.concatenate([v, v], axis=1)
 
-    def in_copy(h, d):
-        return remote(
-            SB.at[h, d], LB.at[h, a], in_send.at[h], in_recv.at[h], member(d)
-        )
-
-    def in_all(h):
-        return remote(
-            SB.at[h, pl.ds(0, M - 1)], LB.at[h, pl.ds(0, M - 1)],
-            in_send.at[h], in_recv.at[h], member(lax.rem(a + 1, M)),
-        )
-
-    def out_copy(h, d):
-        return remote(
-            TB.at[h, d], OB.at[h, a], out_send.at[h], out_recv.at[h], member(d)
+    def left_copy(h, i):
+        return remote(
+            SB.at[h, i, 0], LL.at[h, mine], l_send.at[h], l_recv.at[h], in_half(half, i)
+        )
+
+    def right_copy(par, h, hf, i):
+        return remote(
+            SB.at[h, i, 1], RR.at[par, h, a], i_send.at[h], i_recv.at[par, h], in_half(hf, i)
+        )
+
+    def out_copy(h, i):
+        return remote(
+            TB.at[h, i], OB.at[h, mine], out_send.at[h], out_recv.at[h], in_half(half, i)
+        )
+
+    others = pl.ds(0, MH - 1)
+    everyone = pl.ds(0, M - 1)
+
+    def left_all(h):
+        return remote(
+            LL.at[h, others], LL.at[h, others], l_send.at[h], l_recv.at[h], member(lax.rem(a + 1, M))
+        )
+
+    def right_all(par, h):
+        return remote(
+            RR.at[par, h, everyone], RR.at[par, h, everyone],
+            i_send.at[h], i_recv.at[par, h], member(lax.rem(a + 1, M)),
         )
 
     def out_all(h):
         return remote(
-            TB.at[h, pl.ds(0, M - 1)], OB.at[h, pl.ds(0, M - 1)],
+            TB.at[h, others], OB.at[h, others],
             out_send.at[h], out_recv.at[h], member(lax.rem(a + 1, M)),
         )
 
-    def start_all(copy, h):
+    def start_in(par, h):
         def go(k, c):
-            copy(h, lax.rem(a + k, M)).start()
-            return c
-
-        lax.fori_loop(1, M, go, 0)
+            i = lax.rem(mine + k, MH)
+            j = lax.rem(mine + MH - k, MH)
+            right_copy(par, h, 1 - half, i).start()
+
+            @pl.when(k > 0)
+            def _():
+                left_copy(h, j).start()
+                right_copy(par, h, half, j).start()
+
+            return c
+
+        lax.fori_loop(0, MH, go, 0)
+
+    def start_out(h):
+        def go(k, c):
+            out_copy(h, lax.rem(mine + k, MH)).start()
+            return c
+
+        lax.fori_loop(1, MH, go, 0)
+
+    def in_sent(h):
+        left_all(h).wait_send()
+        right_all(0, h).wait_send()
 
     def pre(l, h):
         g0 = wide(GC[l, 0])
@@ -233,26 +296,30 @@
                 S2R[rows, :] = right[:, e * LANES : (e + 1) * LANES]
             return c
 
-        lax.fori_loop(0, R // 2, project, 0)
+        [project(rp, 0) for rp in range(R // 2)]
 
         @pl.when(l > 0)
         def _():
-            in_all(h).wait_send()
-
-        SB[h, :, 0] = S2L[...].reshape(M, CPO, SUB, LANES).astype(BF16)
-        SB[h, :, 1] = S2R[...].reshape(M, CPO, SUB, LANES).astype(BF16)
-        start_all(in_copy, h)
-        LB[h, a] = SB[h, a]
+            in_sent(h)
+
+        par = l % 2
+        SB[h, :, 0] = S2L[...].reshape(MH, CPO, SUB, LANES).astype(BF16)
+        SB[h, :, 1] = S2R[...].reshape(MH, CPO, SUB, LANES).astype(BF16)
+        start_in(par, h)
+        LL[h, mine] = SB[h, mine, 0]
+        RR[par, h, a] = SB[h, mine, 1]
 
         def gates(rp, c):
             GATE[h, rp] = sigmoid(mm(WPT[l, 4 * C : 5 * C, :], NB[h, rp]))
             return c
 
-        lax.fori_loop(0, R // 2, gates, 0)
+        [gates(rp, 0) for rp in range(R // 2)]
 
     def triangle(l):
+        par = l % 2
         for h in range(2):
-            in_all(h).wait_recv()
+            left_all(h).wait_recv()
+            right_all(par, h).wait_recv()
 
         @pl.when(l > 0)
         def _():
@@ -260,27 +327,27 @@
                 out_all(h).wait_send()
 
         def channel(c, carry):
-            def side(lr):
-                halves = [
-                    LB[h, :, lr, c].astype(F32).reshape(M * SUB, LANES).astype(BF16)
-                    for h in range(2)
-                ]
-                return jnp.concatenate(halves, axis=1)
+            def side(parts):
+                flat = [p.astype(F32).reshape(-1, LANES).astype(BF16) for p in parts]
+                return jnp.concatenate(flat, axis=1)
 
             prod = lax.dot_general(
-                side(0), side(1), (((1,), (1,)), ((), ())), preferred_element_type=F32
+                side([LL[h, :, c] for h in range(2)]),
+                side([RR[par, h, :, c] for h in range(2)]),
+                (((1,), (1,)), ((), ())),
+                preferred_element_type=F32,
             )
             for h in range(2):
                 TB[h, :, c] = (
-                    prod[:, h * LANES : (h + 1) * LANES].reshape(M, SUB, LANES).astype(BF16)
+                    prod[:, h * LANES : (h + 1) * LANES].reshape(MH, SUB, LANES).astype(BF16)
                 )
             return carry
 
         lax.fori_loop(0, CPO, channel, 0)
         for h in range(2):
-            start_all(out_copy, h)
+            start_out(h)
         for h in range(2):
-            OB[h, a] = TB[h, a]
+            OB[h, mine] = TB[h, mine]
 
     def post(l, h):
         out_all(h).wait_recv()
@@ -304,7 +371,7 @@
             ZT[h, rp] = (mid + mm(WDT[l], hidden)).astype(BF16)
             return c
 
-        lax.fori_loop(0, R // 2, update, 0)
+        [update(rp, 0) for rp in range(R // 2)]
 
     def ya_copy(k, h):
         sec = wrap(x + k, S)
@@ -343,21 +410,18 @@
             ya_copy(k, h).start()
         YA[x, h] = ZO[h, pl.ds(E * x, E)]
 
+    w_relay(0)
+    flip_early(0)
     forward(0)
-    flip_early(0)
+    for l in range(1, blocks):
+        w_relay(l)
     gather_in(0)
     pre(0, 0)
     forward(1)
-    w_send_all(0, late)
-    w_send_all(1, early + late)
     gather_in(1)
     pre(0, 1)
 
     def block(l, c):
-        @pl.when(l < blocks - 2)
-        def _():
-            w_send_all(l + 2, early + late)
-
         flip_late(l)
 
         @pl.when(l < blocks - 1)
@@ -406,7 +470,7 @@
             else:
                 o_local(h).start()
     for h in range(2):
-        in_all(h).wait_send()
+        in_sent(h)
         out_all(h).wait_send()
         o_local(h).wait()
         for k in range(1, S):
@@ -416,9 +480,13 @@
             yb_copy(k, h).wait_send()
             o_copy(k, h).wait_send()
             o_copy(k, h).wait_recv()
-    for i in range(len(weights)):
-        for k in range(1, S):
-            w_copy(k, i).wait_send()
+    for turn, which in ((0, early), (1, late)):
+        @pl.when(core == turn)
+        def _():
+            for i in which:
+                for k in range(1, S):
+                    w_copy(k, i).wait_send()
+                    w_relay_copy(wrap(x + k, S), i).wait_send()
 
 
 def per_device(pair_in, crop_mask, proj_weights, out_weights, up_weights, down_weights, norm_gains):
@@ -427,8 +495,10 @@
     MB, R, N, C = pair_in.shape
     FF = up_weights.shape[-1]
     M = S * G
-    CPO = C // M
+    MH = M // 2
+    CPO = C // MH
     E = R // S
+    assert G % 2 == 0
     assert MB == S and R == SUB and N == 2 * LANES and C == LANES and N == R * M
     any_spec = pl.BlockSpec(memory_space=pl.ANY)
     vmem_spec = pl.BlockSpec(memory_space=pltpu.VMEM)
@@ -445,10 +515,11 @@
             V((2, R // 2, C, 2 * LANES), BF16),
             V((2, R // 2, C, 2 * LANES), BF16),
             V((2, R // 2, C, 2 * LANES), F32),
-            V((2, M, 2, CPO, SUB, LANES), BF16),
-            V((2, M, 2, CPO, SUB, LANES), BF16),
-            V((2, M, CPO, SUB, LANES), BF16),
-            V((2, M, CPO, SUB, LANES), BF16),
+            V((2, MH, 2, CPO, SUB, LANES), BF16),
+            V((2, MH, CPO, SUB, LANES), BF16),
+            V((2, 2, M, CPO, SUB, LANES), BF16),
+            V((2, MH, CPO, SUB, LANES), BF16),
+            V((2, MH, CPO, SUB, LANES), BF16),
             V((C * SUB, LANES), F32),
             V((C * SUB, LANES), F32),
             V((C * SUB, LANES), F32),
@@ -468,9 +539,10 @@
             V((S, C, FF), BF16),
             V((S, 3, C, LANES), F32),
         ]
-        + [dma((2,))] * 4
+        + [dma((2,))] * 5
+        + [dma((2, 2))]
         + [dma((S, 2))] * 10
-        + [dma((S, 5))] * 2,
+        + [dma((S, 5))] * 4,
         compiler_params=pltpu.CompilerParams(
             collective_id=0, has_side_effects=True, vmem_limit_bytes=56 * 1024 * 1024
         ),

time: 275 us -> 235 us (0.85); the launches traced: 271 us -> 235 us
  Pallas kernels: 269 us -> 233 us
    pallas_call x1, Pallas kernels: 269 us -> 233 us  [per_device(): pl.pallas_call(functools.partial(kernel, S, G, R, C, FF, S), out_shape=ja...]
where the time goes in v3:
time: 235 us
  Pallas kernels  233 us (99%)
    pallas_call x1, Pallas kernels, per_device(): pl.pallas_call(functools.partial(kernel, S, G, R, C, FF, S), out_shape=ja...  233 us

profile of v3, /device:TPU:34, one launch (start us, length us, event | category | flops | bytes accessed | tf_op | source)
XLA Modules:
  0.0 235.3 jit_solution(3723603096762869586)
XLA Ops:
  0.0 233.4 %shard_map.73 = bf16[1,8,256,128]{3,2,1,0:T(8,128)(2,1)} custom-call(bf16[4,8,256,128]{3,2,1,0:T(8,128)(2,1)} %pair_ref.1, s32[4,256]{1,0:T(4,128)} %mask_ref.1, bf16[1,5,128,128]{3,2,1,0:T(8,128)(2,1)} %proj_ref.1, bf16[1,128,128]{2,1,0:T(8,128)(2,1)} %wout_ref.1, bf16[1,128,512]{2,1,0:T(8,128)(2,1)} %up_ref.1, bf16[1,512,128]{2,1,0:T(8,128)(2,1)} %down_ref.1, ...), custom_call_target="tpu_custom_call" | custom-call | tf_op jit(solution)/shard_map/pallas_call | solution.py:507
  233.4 1.9 copy.9

commit v4 on v3

--- a/solution.py
+++ b/solution.py
@@ -33,11 +33,10 @@
     S, G, R, C, FF, blocks,
     pair_ref, mask_ref, proj_ref, wout_ref, up_ref, down_ref, gain_ref,
     out_ref,
-    XB, ZIN, ZT, NB, GATE, SB, LL, RR, TB, OB, S2L, S2R, S3, RS, PM, ZO, YA, YB,
+    ZIN, ZT, NB, GATE, SB, LL, RR, TB, OB, S2L, S2R, S3, RS, PM, ZO, YA,
     WP, WO, WU, WD, GN, WPT, WOT, WUT, WDT, GC,
     l_send, l_recv, i_send, out_send, out_recv, i_recv,
-    xb_send, xb_recv, z_send, z_recv,
-    ya_send, ya_recv, yb_send, yb_recv, o_send, o_recv,
+    z_send, z_recv, ya_send, ya_recv, o_send, o_recv,
     w_send, w_recv, r_send, r_recv,
 ):
     M = S * G
@@ -62,9 +61,6 @@
     def in_half(hf, i):
         return {"section": lax.div(i, GH), "axial": m * G + hf * GH + lax.rem(i, GH)}
 
-    def along_z(seg):
-        return {"section": x, "axial": seg * G + t}
-
     def along_x(sec):
         return {"section": sec, "axial": A}
 
@@ -83,25 +79,42 @@
         return c
 
     lax.fori_loop(1, M, greet, 0)
-    for k in range(1, S):
-        pl.semaphore_signal(
-            barrier, inc=1, device_id=along_z(wrap(m + k, S)), device_id_type=MESH
-        )
+    @pl.when(x != m)
+    def _():
+        for sec in range(S):
+            pl.semaphore_signal(
+                barrier, inc=1, device_id={"section": sec, "axial": x * G + t},
+                device_id_type=MESH,
+            )
+
     pl.semaphore_wait(barrier, M - 1 + S - 1)
 
-    def xb_copy(k, h):
+    def home(seg):
+        return {"section": m, "axial": seg * G + t}
+
+    def piece(ref, row, h):
+        return ref.at[row, pl.ds(E * x, E), pl.ds(h * LANES, LANES), :]
+
+    def z_copy(k, h):
         dest = wrap(m + k, S)
         return remote(
-            pair_ref.at[dest, pl.ds(E * x, E), pl.ds(h * LANES, LANES), :],
-            XB.at[m, h],
-            xb_send.at[k, h], xb_recv.at[k, h], along_z(dest),
-        )
-
-    def xb_local(h):
-        return pltpu.make_async_copy(
-            pair_ref.at[m, pl.ds(E * x, E), pl.ds(h * LANES, LANES), :],
-            XB.at[m, h], xb_recv.at[0, h],
-        )
+            piece(pair_ref, dest, h), ZIN.at[h, pl.ds(E * x, E)],
+            z_send.at[k, h], z_recv.at[x, h], home(dest),
+        )
+
+    def z_start(k, h):
+        if k:
+            z_copy(k, h).start()
+        else:
+            @pl.when(x != m)
+            def _():
+                z_copy(0, h).start()
+
+            @pl.when(x == m)
+            def _():
+                pltpu.make_async_copy(
+                    piece(pair_ref, m, h), ZIN.at[h, pl.ds(E * x, E)], z_recv.at[x, h]
+                ).start()
 
     weights = ((proj_ref, WP), (wout_ref, WO), (up_ref, WU), (down_ref, WD), (gain_ref, GN))
 
@@ -150,9 +163,8 @@
     early, late = (0, 4), (1, 2, 3)
     order = (S // 2,) + tuple(k for k in range(1, S) if k != S // 2)
     for h in range(2):
-        for k in order:
-            xb_copy(k, h).start()
-        xb_local(h).start()
+        for k in order + (0,):
+            z_start(k, h)
     for i in early + late:
         w_local(i).start()
     for turn, which in ((0, early), (1, late)):
@@ -188,26 +200,10 @@
             WUT[l, f * C : (f + 1) * C, :] = flip(WU[l, :, f * C : (f + 1) * C])
             WDT[l, :, f * C : (f + 1) * C] = flip(WD[l, f * C : (f + 1) * C, :])
 
-    def z_copy(k, h):
-        sec = wrap(x + k, S)
-        return remote(
-            XB.at[sec, h], ZIN.at[h, pl.ds(E * x, E)],
-            z_send.at[k, h], z_recv.at[k, h], along_x(sec),
-        )
-
-    def forward(h):
-        for k in order + (0,):
-            sec = wrap(x + k, S)
-            kz = wrap(m - sec, S)
-            pltpu.make_async_copy(XB.at[sec, h], XB.at[sec, h], xb_recv.at[kz, h]).wait()
-            if k:
-                z_copy(k, h).start()
-            else:
-                ZIN[h, pl.ds(E * x, E)] = XB[x, h]
-
     def gather_in(h):
-        for k in range(1, S):
-            z_copy(k, h).wait_recv()
+        for sec in range(S):
+            rows = ZIN.at[h, pl.ds(E * sec, E)]
+            pltpu.make_async_copy(rows, rows, z_recv.at[sec, h]).wait()
 
         def turn(rp, c):
             parts = [ZIN[h, 2 * rp + e].astype(F32).T for e in range(2)]
@@ -219,9 +215,9 @@
     def wide(v):
         return jnp.concatenate([v, v], axis=1)
 
-    def left_copy(h, i):
-        return remote(
-            SB.at[h, i, 0], LL.at[h, mine], l_send.at[h], l_recv.at[h], in_half(half, i)
+    def left_copy(par, h, i):
+        return remote(
+            SB.at[h, i, 0], LL.at[par, h, mine], l_send.at[h], l_recv.at[h], in_half(half, i)
         )
 
     def right_copy(par, h, hf, i):
@@ -239,7 +235,7 @@
 
     def left_all(h):
         return remote(
-            LL.at[h, others], LL.at[h, others], l_send.at[h], l_recv.at[h], member(lax.rem(a + 1, M))
+            LL.at[0, h, others], LL.at[0, h, others], l_send.at[h], l_recv.at[h], member(lax.rem(a + 1, M))
         )
 
     def right_all(par, h):
@@ -262,7 +258,7 @@
 
             @pl.when(k > 0)
             def _():
-                left_copy(h, j).start()
+                left_copy(par, h, j).start()
                 right_copy(par, h, half, j).start()
 
             return c
@@ -306,7 +302,7 @@
         SB[h, :, 0] = S2L[...].reshape(MH, CPO, SUB, LANES).astype(BF16)
         SB[h, :, 1] = S2R[...].reshape(MH, CPO, SUB, LANES).astype(BF16)
         start_in(par, h)
-        LL[h, mine] = SB[h, mine, 0]
+        LL[par, h, mine] = SB[h, mine, 0]
         RR[par, h, a] = SB[h, mine, 1]
 
         def gates(rp, c):
@@ -326,27 +322,23 @@
             for h in range(2):
                 out_all(h).wait_send()
 
-        def channel(c, carry):
-            def side(parts):
-                flat = [p.astype(F32).reshape(-1, LANES).astype(BF16) for p in parts]
-                return jnp.concatenate(flat, axis=1)
-
-            prod = lax.dot_general(
-                side([LL[h, :, c] for h in range(2)]),
-                side([RR[par, h, :, c] for h in range(2)]),
-                (((1,), (1,)), ((), ())),
-                preferred_element_type=F32,
-            )
-            for h in range(2):
-                TB[h, :, c] = (
-                    prod[:, h * LANES : (h + 1) * LANES].reshape(MH, SUB, LANES).astype(BF16)
+        def side(parts):
+            flat = [p.astype(F32).reshape(-1, LANES).astype(BF16) for p in parts]
+            return jnp.concatenate(flat, axis=1)
+
+        for h in range(2):
+            def channel(c, carry):
+                prod = lax.dot_general(
+                    side([LL[par, e, :, c] for e in range(2)]),
+                    side([RR[par, e, h * MH : (h + 1) * MH, c] for e in range(2)]),
+                    (((1,), (1,)), ((), ())),
+                    preferred_element_type=F32,
                 )
-            return carry
-
-        lax.fori_loop(0, CPO, channel, 0)
-        for h in range(2):
+                TB[h, :, c] = prod.reshape(MH, SUB, LANES).astype(BF16)
+                return carry
+
+            lax.fori_loop(0, CPO, channel, 0, unroll=2)
             start_out(h)
-        for h in range(2):
             OB[h, mine] = TB[h, mine]
 
     def post(l, h):
@@ -380,23 +372,11 @@
             ya_send.at[k, h], ya_recv.at[k, h], along_x(sec),
         )
 
-    def yb_copy(k, h):
+    def o_copy(k, h):
         seg = wrap(m + k, S)
         return remote(
-            YA.at[seg, h], YB.at[m, h], yb_send.at[k, h], yb_recv.at[k, h], along_z(seg)
-        )
-
-    def o_slice(h):
-        return out_ref.at[0, pl.ds(E * x, E), pl.ds(h * LANES, LANES), :]
-
-    def o_copy(k, h):
-        sec = wrap(x + k, S)
-        return remote(
-            YB.at[sec, h], o_slice(h), o_send.at[k, h], o_recv.at[k, h], along_x(sec)
-        )
-
-    def o_local(h):
-        return pltpu.make_async_copy(YB.at[x, h], o_slice(h), o_recv.at[0, h])
+            YA.at[seg, h], piece(out_ref, 0, h), o_send.at[k, h], o_recv.at[x, h], home(seg)
+        )
 
     def spread(h):
         def turn_back(rp, c):
@@ -412,12 +392,10 @@
 
     w_relay(0)
     flip_early(0)
-    forward(0)
+    gather_in(0)
+    pre(0, 0)
     for l in range(1, blocks):
         w_relay(l)
-    gather_in(0)
-    pre(0, 0)
-    forward(1)
     gather_in(1)
     pre(0, 1)
 
@@ -453,33 +431,34 @@
                 pltpu.make_async_copy(YA.at[seg, h], YA.at[seg, h], ya_recv.at[kx, h]).wait()
 
             if k:
-                yb_copy(k, h).start()
-            else:
-                YB[m, h] = YA[m, h]
-    for h in range(2):
-        for k in order + (0,):
-            sec = wrap(x + k, S)
-            kz = wrap(m - sec, S)
-
-            @pl.when(kz != 0)
-            def _():
-                pltpu.make_async_copy(YB.at[sec, h], YB.at[sec, h], yb_recv.at[kz, h]).wait()
-
-            if k:
                 o_copy(k, h).start()
             else:
-                o_local(h).start()
+                @pl.when(x != m)
+                def _():
+                    o_copy(0, h).start()
+
+                @pl.when(x == m)
+                def _():
+                    pltpu.make_async_copy(
+                        YA.at[m, h], piece(out_ref, 0, h), o_recv.at[x, h]
+                    ).start()
+
     for h in range(2):
         in_sent(h)
         out_all(h).wait_send()
-        o_local(h).wait()
+        for sec in range(S):
+            rows = out_ref.at[0, pl.ds(E * sec, E), pl.ds(h * LANES, LANES), :]
+            pltpu.make_async_copy(rows, rows, o_recv.at[sec, h]).wait()
         for k in range(1, S):
-            xb_copy(k, h).wait_send()
             z_copy(k, h).wait_send()
             ya_copy(k, h).wait_send()
-            yb_copy(k, h).wait_send()
             o_copy(k, h).wait_send()
-            o_copy(k, h).wait_recv()
+
+        @pl.when(x != m)
+        def _():
+            z_copy(0, h).wait_send()
+            o_copy(0, h).wait_send()
+
     for turn, which in ((0, early), (1, late)):
         @pl.when(core == turn)
         def _():
@@ -510,13 +489,12 @@
         in_specs=[any_spec, vmem_spec] + [any_spec] * 5,
         out_specs=any_spec,
         scratch_shapes=[
-            V((S, 2, E, LANES, C), BF16),
             V((2, R, LANES, C), BF16),
             V((2, R // 2, C, 2 * LANES), BF16),
             V((2, R // 2, C, 2 * LANES), BF16),
             V((2, R // 2, C, 2 * LANES), F32),
             V((2, MH, 2, CPO, SUB, LANES), BF16),
-            V((2, MH, CPO, SUB, LANES), BF16),
+            V((2, 2, MH, CPO, SUB, LANES), BF16),
             V((2, 2, M, CPO, SUB, LANES), BF16),
             V((2, MH, CPO, SUB, LANES), BF16),
             V((2, MH, CPO, SUB, LANES), BF16),
@@ -526,7 +504,6 @@
             V((SUB, LANES), F32),
             V((2, SUB, LANES), F32),
             V((2, R, LANES, C), BF16),
-            V((S, 2, E, LANES, C), BF16),
             V((S, 2, E, LANES, C), BF16),
             V((S, 5, C, C), BF16),
             V((S, C, C), BF16),
@@ -541,7 +518,7 @@
         ]
         + [dma((2,))] * 5
         + [dma((2, 2))]
-        + [dma((S, 2))] * 10
+        + [dma((S, 2))] * 6
         + [dma((S, 5))] * 4,
         compiler_params=pltpu.CompilerParams(
             collective_id=0, has_side_effects=True, vmem_limit_bytes=56 * 1024 * 1024

time: 235 us -> 223 us (0.949)
  Pallas kernels: 233 us -> 220 us
    pallas_call x1, Pallas kernels: 233 us -> 220 us  [per_device(): pl.pallas_call(functools.partial(kernel, S, G, R, C, FF, S), out_shape=ja...]
where the time goes in v4:
time: 223 us; the launch traced here: 222 us
  Pallas kernels  220 us (99%)
    pallas_call x1, Pallas kernels, per_device(): pl.pallas_call(functools.partial(kernel, S, G, R, C, FF, S), out_shape=ja...  220 us

profile of v4, /device:TPU:34, one launch (start us, length us, event | category | flops | bytes accessed | tf_op | source)
XLA Modules:
  0.0 222.0 jit_solution(10484218568789240156)
XLA Ops:
  0.0 220.1 %shard_map.73 = bf16[1,8,256,128]{3,2,1,0:T(8,128)(2,1)} custom-call(bf16[4,8,256,128]{3,2,1,0:T(8,128)(2,1)} %pair_ref.1, s32[4,256]{1,0:T(4,128)} %mask_ref.1, bf16[1,5,128,128]{3,2,1,0:T(8,128)(2,1)} %proj_ref.1, bf16[1,128,128]{2,1,0:T(8,128)(2,1)} %wout_ref.1, bf16[1,128,512]{2,1,0:T(8,128)(2,1)} %up_ref.1, bf16[1,512,128]{2,1,0:T(8,128)(2,1)} %down_ref.1, ...), custom_call_target="tpu_custom_call" | custom-call | tf_op jit(solution)/shard_map/pallas_call | solution.py:486
  220.1 1.9 copy.9

commit v5 on v4

--- a/solution.py
+++ b/solution.py
@@ -33,7 +33,7 @@
     S, G, R, C, FF, blocks,
     pair_ref, mask_ref, proj_ref, wout_ref, up_ref, down_ref, gain_ref,
     out_ref,
-    ZIN, ZT, NB, GATE, SB, LL, RR, TB, OB, S2L, S2R, S3, RS, PM, ZO, YA,
+    ZIN, ZT, NB, GATE, SB, LL, RR, PART, TB, OB, S2L, S2R, S3, RS, PM, ZO, YA,
     WP, WO, WU, WD, GN, WPT, WOT, WUT, WDT, GC,
     l_send, l_recv, i_send, out_send, out_recv, i_recv,
     z_send, z_recv, ya_send, ya_recv, o_send, o_recv,
@@ -78,7 +78,6 @@
         )
         return c
 
-    lax.fori_loop(1, M, greet, 0)
     @pl.when(x != m)
     def _():
         for sec in range(S):
@@ -87,6 +86,7 @@
                 device_id_type=MESH,
             )
 
+    lax.fori_loop(1, M, greet, 0)
     pl.semaphore_wait(barrier, M - 1 + S - 1)
 
     def home(seg):
@@ -313,31 +313,41 @@
 
     def triangle(l):
         par = l % 2
-        for h in range(2):
-            left_all(h).wait_recv()
-            right_all(par, h).wait_recv()
+
+        def flat(v):
+            return v.astype(F32).reshape(-1, LANES).astype(BF16)
+
+        def outer(p, q):
+            return lax.dot_general(
+                flat(p), flat(q), (((1,), (1,)), ((), ())), preferred_element_type=F32
+            )
+
+        def arrived(e):
+            left_all(e).wait_recv()
+            right_all(par, e).wait_recv()
+
+        def first(c, carry):
+            PART[c] = outer(LL[par, 0, :, c], RR[par, 0, :, c])
+            return carry
+
+        arrived(0)
+        lax.fori_loop(0, CPO, first, 0, unroll=2)
 
         @pl.when(l > 0)
         def _():
             for h in range(2):
                 out_all(h).wait_send()
 
-        def side(parts):
-            flat = [p.astype(F32).reshape(-1, LANES).astype(BF16) for p in parts]
-            return jnp.concatenate(flat, axis=1)
-
+        arrived(1)
         for h in range(2):
             def channel(c, carry):
-                prod = lax.dot_general(
-                    side([LL[par, e, :, c] for e in range(2)]),
-                    side([RR[par, e, h * MH : (h + 1) * MH, c] for e in range(2)]),
-                    (((1,), (1,)), ((), ())),
-                    preferred_element_type=F32,
+                prod = PART[c, :, h * LANES : (h + 1) * LANES] + outer(
+                    LL[par, 1, :, c], RR[par, 1, h * MH : (h + 1) * MH, c]
                 )
                 TB[h, :, c] = prod.reshape(MH, SUB, LANES).astype(BF16)
                 return carry
 
-            lax.fori_loop(0, CPO, channel, 0, unroll=2)
+            lax.fori_loop(0, CPO, channel, 0, unroll=True)
             start_out(h)
             OB[h, mine] = TB[h, mine]
 
@@ -496,6 +506,7 @@
             V((2, MH, 2, CPO, SUB, LANES), BF16),
             V((2, 2, MH, CPO, SUB, LANES), BF16),
             V((2, 2, M, CPO, SUB, LANES), BF16),
+            V((CPO, MH * SUB, 2 * LANES), F32),
             V((2, MH, CPO, SUB, LANES), BF16),
             V((2, MH, CPO, SUB, LANES), BF16),
             V((C * SUB, LANES), F32),

time: 223 us -> 221 us (level)
  Pallas kernels: 220 us -> 217 us
    pallas_call x1, Pallas kernels: 220 us -> 217 us  [per_device(): pl.pallas_call(functools.partial(kernel, S, G, R, C, FF, S), out_shape=ja...]
where the time goes in v5:
time: 221 us; the launch traced here: 219 us
  Pallas kernels  217 us (98%)
    pallas_call x1, Pallas kernels, per_device(): pl.pallas_call(functools.partial(kernel, S, G, R, C, FF, S), out_shape=ja...  217 us

profile of v5, /device:TPU:34, one launch (start us, length us, event | category | flops | bytes accessed | tf_op | source)
XLA Modules:
  0.0 219.1 jit_solution(13586677312385952279)
XLA Ops:
  0.0 217.2 %shard_map.73 = bf16[1,8,256,128]{3,2,1,0:T(8,128)(2,1)} custom-call(bf16[4,8,256,128]{3,2,1,0:T(8,128)(2,1)} %pair_ref.1, s32[4,256]{1,0:T(4,128)} %mask_ref.1, bf16[1,5,128,128]{3,2,1,0:T(8,128)(2,1)} %proj_ref.1, bf16[1,128,128]{2,1,0:T(8,128)(2,1)} %wout_ref.1, bf16[1,128,512]{2,1,0:T(8,128)(2,1)} %up_ref.1, bf16[1,512,128]{2,1,0:T(8,128)(2,1)} %down_ref.1, ...), custom_call_target="tpu_custom_call" | custom-call | tf_op jit(solution)/shard_map/pallas_call | solution.py:496
  217.2 1.9 copy.9

commit v6 on v5

--- a/solution.py
+++ b/solution.py
@@ -205,12 +205,13 @@
             rows = ZIN.at[h, pl.ds(E * sec, E)]
             pltpu.make_async_copy(rows, rows, z_recv.at[sec, h]).wait()
 
-        def turn(rp, c):
+        for rp in range(R // 2):
             parts = [ZIN[h, 2 * rp + e].astype(F32).T for e in range(2)]
-            ZT[h, rp] = jnp.concatenate(parts, axis=1).astype(BF16)
-            return c
-
-        lax.fori_loop(0, R // 2, turn, 0)
+            turned = jnp.concatenate(parts, axis=1).astype(BF16)
+            ZT[h, rp] = turned
+            project(0, h, rp, turned.astype(F32))
+
+        send_edges(0, h)
 
     def wide(v):
         return jnp.concatenate([v, v], axis=1)
@@ -276,24 +277,19 @@
         left_all(h).wait_send()
         right_all(0, h).wait_send()
 
-    def pre(l, h):
-        g0 = wide(GC[l, 0])
-
-        def project(rp, c):
-            normed = (norm_rows(ZT[h, rp].astype(F32)) * g0).astype(BF16)
-            NB[h, rp] = normed
-            lin = mm(WPT[l, 0 : 4 * C, :], normed)
-            pm = jnp.concatenate([PM[h, pl.ds(2 * rp, 1), :], PM[h, pl.ds(2 * rp + 1, 1), :]], axis=1)
-            left = sigmoid(lin[C : 2 * C]) * lin[0:C] * pm
-            right = sigmoid(lin[3 * C : 4 * C]) * lin[2 * C : 3 * C] * pm
-            for e in range(2):
-                rows = pl.ds(2 * rp + e, C, stride=SUB)
-                S2L[rows, :] = left[:, e * LANES : (e + 1) * LANES]
-                S2R[rows, :] = right[:, e * LANES : (e + 1) * LANES]
-            return c
-
-        [project(rp, 0) for rp in range(R // 2)]
-
+    def project(l, h, rp, z):
+        normed = (norm_rows(z) * wide(GC[l, 0])).astype(BF16)
+        NB[h, rp] = normed
+        lin = mm(WPT[l, 0 : 4 * C, :], normed)
+        pm = jnp.concatenate([PM[h, pl.ds(2 * rp + e, 1), :] for e in range(2)], axis=1)
+        left = sigmoid(lin[C : 2 * C]) * lin[0:C] * pm
+        right = sigmoid(lin[3 * C : 4 * C]) * lin[2 * C : 3 * C] * pm
+        for e in range(2):
+            rows = pl.ds(2 * rp + e, C, stride=SUB)
+            S2L[rows, :] = left[:, e * LANES : (e + 1) * LANES]
+            S2R[rows, :] = right[:, e * LANES : (e + 1) * LANES]
+
+    def send_edges(l, h):
         @pl.when(l > 0)
         def _():
             in_sent(h)
@@ -351,7 +347,7 @@
             start_out(h)
             OB[h, mine] = TB[h, mine]
 
-    def post(l, h):
+    def post(l, h, follow):
         out_all(h).wait_recv()
         got = OB[h].astype(F32).reshape(C, SUB, LANES)
         mean = jnp.sum(got, axis=0) * (1.0 / C)
@@ -361,7 +357,7 @@
         g1 = wide(GC[l, 1])
         g2 = wide(GC[l, 2])
 
-        def update(rp, c):
+        for rp in range(R // 2):
             vals = jnp.concatenate(
                 [S3[pl.ds(2 * rp + e, C, stride=SUB), :] for e in range(2)], axis=1
             )
@@ -370,10 +366,11 @@
             mid = ZT[h, rp].astype(F32) + GATE[h, rp] * mm(WOT[l], tri_norm)
             trans_in = (norm_rows(mid) * g2).astype(BF16)
             hidden = jnp.maximum(mm(WUT[l], trans_in), 0.0).astype(BF16)
-            ZT[h, rp] = (mid + mm(WDT[l], hidden)).astype(BF16)
-            return c
-
-        [update(rp, 0) for rp in range(R // 2)]
+            new = (mid + mm(WDT[l], hidden)).astype(BF16)
+            ZT[h, rp] = new
+            if follow:
+                project(l + 1, h, rp, new.astype(F32))
+
 
     def ya_copy(k, h):
         sec = wrap(x + k, S)
@@ -389,13 +386,10 @@
         )
 
     def spread(h):
-        def turn_back(rp, c):
+        for rp in range(R // 2):
             v = ZT[h, rp].astype(F32)
             for e in range(2):
                 ZO[h, 2 * rp + e] = v[:, e * LANES : (e + 1) * LANES].T.astype(BF16)
-            return c
-
-        lax.fori_loop(0, R // 2, turn_back, 0)
         for k in order:
             ya_copy(k, h).start()
         YA[x, h] = ZO[h, pl.ds(E * x, E)]
@@ -403,34 +397,26 @@
     w_relay(0)
     flip_early(0)
     gather_in(0)
-    pre(0, 0)
     for l in range(1, blocks):
         w_relay(l)
     gather_in(1)
-    pre(0, 1)
 
     def block(l, c):
         flip_late(l)
-
-        @pl.when(l < blocks - 1)
-        def _():
-            flip_early(l + 1)
-
+        flip_early(l + 1)
         triangle(l)
         for h in range(2):
-            post(l, h)
-
-            @pl.when(l < blocks - 1)
-            def _():
-                pre(l + 1, h)
-
-            @pl.when(l == blocks - 1)
-            def _():
-                spread(h)
-
+            post(l, h, True)
+            send_edges(l + 1, h)
         return c
 
-    lax.fori_loop(0, blocks, block, 0)
+    lax.fori_loop(0, blocks - 1, block, 0)
+    flip_late(blocks - 1)
+    triangle(blocks - 1)
+    for h in range(2):
+        post(blocks - 1, h, False)
+        spread(h)
+
     for h in range(2):
         for k in order + (0,):
             seg = wrap(m + k, S)

time: 221 us -> 219 us (level)
  no operation moved by 1% of the time
where the time goes in v6:
time: 219 us; the launch traced here: 218 us
  Pallas kernels  217 us (99%)
    pallas_call x1, Pallas kernels, per_device(): pl.pallas_call(functools.partial(kernel, S, G, R, C, FF, S), out_shape=ja...  217 us

profile of v6, /device:TPU:34, one launch (start us, length us, event | category | flops | bytes accessed | tf_op | source)
XLA Modules:
  0.0 218.4 jit_solution(686095674024541135)
XLA Ops:
  0.0 216.6 %shard_map.73 = bf16[1,8,256,128]{3,2,1,0:T(8,128)(2,1)} custom-call(bf16[4,8,256,128]{3,2,1,0:T(8,128)(2,1)} %pair_ref.1, s32[4,256]{1,0:T(4,128)} %mask_ref.1, bf16[1,5,128,128]{3,2,1,0:T(8,128)(2,1)} %proj_ref.1, bf16[1,128,128]{2,1,0:T(8,128)(2,1)} %wout_ref.1, bf16[1,128,512]{2,1,0:T(8,128)(2,1)} %up_ref.1, bf16[1,512,128]{2,1,0:T(8,128)(2,1)} %down_ref.1, ...), custom_call_target="tpu_custom_call" | custom-call | tf_op jit(solution)/shard_map/pallas_call | solution.py:482
  216.6 1.9 copy.9

commit v7 on v6

--- a/solution.py
+++ b/solution.py
@@ -394,6 +394,28 @@
             ya_copy(k, h).start()
         YA[x, h] = ZO[h, pl.ds(E * x, E)]
 
+    def place(h):
+        for k in order + (0,):
+            seg = wrap(m + k, S)
+            kx = wrap(x - seg, S)
+
+            @pl.when(kx != 0)
+            def _():
+                pltpu.make_async_copy(YA.at[seg, h], YA.at[seg, h], ya_recv.at[kx, h]).wait()
+
+            if k:
+                o_copy(k, h).start()
+            else:
+                @pl.when(x != m)
+                def _():
+                    o_copy(0, h).start()
+
+                @pl.when(x == m)
+                def _():
+                    pltpu.make_async_copy(
+                        YA.at[m, h], piece(out_ref, 0, h), o_recv.at[x, h]
+                    ).start()
+
     w_relay(0)
     flip_early(0)
     gather_in(0)
@@ -413,31 +435,12 @@
     lax.fori_loop(0, blocks - 1, block, 0)
     flip_late(blocks - 1)
     triangle(blocks - 1)
-    for h in range(2):
-        post(blocks - 1, h, False)
-        spread(h)
-
-    for h in range(2):
-        for k in order + (0,):
-            seg = wrap(m + k, S)
-            kx = wrap(x - seg, S)
-
-            @pl.when(kx != 0)
-            def _():
-                pltpu.make_async_copy(YA.at[seg, h], YA.at[seg, h], ya_recv.at[kx, h]).wait()
-
-            if k:
-                o_copy(k, h).start()
-            else:
-                @pl.when(x != m)
-                def _():
-                    o_copy(0, h).start()
-
-                @pl.when(x == m)
-                def _():
-                    pltpu.make_async_copy(
-                        YA.at[m, h], piece(out_ref, 0, h), o_recv.at[x, h]
-                    ).start()
+    post(blocks - 1, 0, False)
+    spread(0)
+    post(blocks - 1, 1, False)
+    place(0)
+    spread(1)
+    place(1)
 
     for h in range(2):
         in_sent(h)

time: 219 us -> 218 us (level)
  no operation moved by 1% of the time
where the time goes in v7:
time: 218 us
  Pallas kernels  216 us (99%)
    pallas_call x1, Pallas kernels, per_device(): pl.pallas_call(functools.partial(kernel, S, G, R, C, FF, S), out_shape=ja...  216 us

profile of v7, /device:TPU:34, one launch (start us, length us, event | category | flops | bytes accessed | tf_op | source)
XLA Modules:
  0.0 217.9 jit_solution(16300615560047071395)
XLA Ops:
  0.0 216.0 %shard_map.73 = bf16[1,8,256,128]{3,2,1,0:T(8,128)(2,1)} custom-call(bf16[4,8,256,128]{3,2,1,0:T(8,128)(2,1)} %pair_ref.1, s32[4,256]{1,0:T(4,128)} %mask_ref.1, bf16[1,5,128,128]{3,2,1,0:T(8,128)(2,1)} %proj_ref.1, bf16[1,128,128]{2,1,0:T(8,128)(2,1)} %wout_ref.1, bf16[1,128,512]{2,1,0:T(8,128)(2,1)} %up_ref.1, bf16[1,512,128]{2,1,0:T(8,128)(2,1)} %down_ref.1, ...), custom_call_target="tpu_custom_call" | custom-call | tf_op jit(solution)/shard_map/pallas_call | solution.py:485
  216.0 1.9 copy.9
